TPU v7x, 32 devices: a whole 2x2x4 slice. The times are simulated.
32 devices in a mesh: row: 8 (over z, y), col: 4 (over x, core).
Axes of the slice: x: 2, y: 2, z: 4, core: 2. Of those that a mesh axis runs over, the one named last changes fastest.
Arguments:
- grads: float32 [64, 20, 3, 4096], P(None, None, None, ('row', 'col')), may hold values from -6 to 6
- weights: float32 [64, 4096], P(None, ('row', 'col')), may hold values from 0.005 to 0.05
- counts: int32 [4096], P(('row', 'col')), may hold values from 1 to 8
- lame_first: float32 [4096], P(('row', 'col')), may hold values from 0.5 to 2
- shear: float32 [4096], P(('row', 'col')), may hold values from 0.5 to 2
- dest_owner: int32 [4096, 1], P(('row', 'col')), may hold values from 0 to 31; in each aligned block of 128 rows (0 to 127, 128 to 255, ...) at most 8 rows name the same one
- dest_slot: int32 [4096], P(('row', 'col')), may hold values from 0 to 127
Outputs:
- assembled: float32 [60, 60, 4096], P(None, None, ('row', 'col'))
Inputs may be any that keep to these rules, and one draw needn't show every extreme that they name: `dest_owner`: among the elements of one device, at most 8 have the same owner; in some device exactly 8 do.
All inputs are finite; a program needn't handle non-finite values.
Results may differ from a plain program's by a relative error of at most 0.0001.
Values sent between devices are 32-bit elements; how exact they have to be, the bound alone decides.
A program may use at most 64 MiB of HBM per device.

v0:
```python
import jax
import jax.numpy as jnp
import numpy as np
from jax import lax
from jax.sharding import PartitionSpec as P

NF = 20
NDOF = 60
GP = 8
Q = 64
SLOTS_DEV = 128


def stiffness(gflat, weff, lame_first, shear):
    count = gflat.shape[2]
    moment = jnp.einsum(
        "qme,qne->mne", gflat * weff[:, None, :], gflat, precision=lax.Precision.HIGHEST
    )
    blocks = moment.reshape(NF, 3, NF, 3, count)
    across = jnp.einsum("akbke->abe", blocks)
    eye = jnp.eye(3, dtype=jnp.float32)
    result = lame_first * blocks + shear * (
        eye[None, :, None, :, None] * across[:, None, :, None, :]
        + jnp.transpose(blocks, (0, 3, 2, 1, 4))
    )
    return result.reshape(NDOF * NDOF, count)


def triangle_tables(order):
    upper_rows, upper_cols = np.triu_indices(order)
    lookup = np.zeros((order, order), np.int32)
    lookup[upper_rows, upper_cols] = np.arange(upper_rows.shape[0], dtype=np.int32)
    lookup[upper_cols, upper_rows] = np.arange(upper_rows.shape[0], dtype=np.int32)
    upper_index = (upper_rows * order + upper_cols).astype(np.int32)
    return (upper_index, lookup.reshape(order * order))


def deliver(payload, slotcol):
    return (
        lax.all_to_all(payload, ("row", "col"), split_axis=1, concat_axis=1, tiled=True),
        lax.all_to_all(slotcol, ("row", "col"), split_axis=1, concat_axis=1, tiled=True),
    )


def shards(grads, weights, counts, lame_first, shear, dest_owner, dest_slot):
    count = grads.shape[3]
    nrow = lax.axis_size("row")
    ncol = lax.axis_size("col")
    ndevices = nrow * ncol
    capacity = max(2, 2 * count // ndevices)
    width = ndevices * capacity
    points = lax.broadcasted_iota(jnp.int32, weights.shape, 0)
    weff = jnp.where(points < counts[None, :] * GP, weights, jnp.float32(0.0))
    squares = jnp.sum(grads * grads, axis=(1, 2))
    local_trace = jnp.sum((lame_first + 4.0 * shear) * jnp.sum(weff * squares, axis=0))
    total = lax.psum(local_trace, ("row", "col"))
    scale = total / (NDOF * count * ndevices)
    owner = dest_owner[:, 0]
    onehot = (owner[:, None] == lax.broadcasted_iota(jnp.int32, (count, ndevices), 1)).astype(
        jnp.int32
    )
    ranking = jnp.sum(jnp.cumsum(onehot, axis=0) * onehot, axis=1) - 1
    position = owner * capacity + ranking
    slotcol = (
        jnp.full((1, width), -1.0, jnp.float32).at[0, position].set(dest_slot.astype(jnp.float32))
    )
    gflat = grads.reshape(Q, NDOF, count)
    upper_index, mirror_index = triangle_tables(NDOF)
    local_blocks = stiffness(gflat, weff, lame_first, shear)
    upper_part = jnp.take(local_blocks, jnp.asarray(upper_index, jnp.int32), axis=0)
    payload = jnp.zeros((upper_part.shape[0], width), jnp.float32).at[:, position].set(upper_part)
    moved, slots_in = deliver(payload, slotcol)
    received = jnp.take(moved, jnp.asarray(mirror_index, jnp.int32), axis=0)
    slot_ids = slots_in[0].astype(jnp.int32)
    placing = (slot_ids[:, None] == lax.broadcasted_iota(jnp.int32, (width, SLOTS_DEV), 1)).astype(
        jnp.float32
    )
    summed = jnp.dot(
        received, placing, precision=lax.Precision.HIGHEST, preferred_element_type=jnp.float32
    )
    return (summed / scale).reshape(NDOF, NDOF, SLOTS_DEV)


def solution(mesh):
    in_specs = (
        P(None, None, None, ("row", "col")),
        P(None, ("row", "col")),
        P(("row", "col")),
        P(("row", "col")),
        P(("row", "col")),
        P(("row", "col"), None),
        P(("row", "col")),
    )
    out_specs = P(None, None, ("row", "col"))
    return jax.shard_map(shards, mesh=mesh, in_specs=in_specs, out_specs=out_specs, check_vma=False)
```

profile of v0, /device:TPU:0, one launch (start us, length us, event | category | flops | bytes accessed | tf_op | source)
XLA Modules:
  0.0 143.4 jit_solution(12971024460196947275)
XLA Ops:
  0.0 0.9 fusion.11
  0.9 0.2 reduce_window_sum.11
  1.1 0.8 select_reduce_fusion.1
  1.9 0.7 fusion.14
  2.6 0.7 convert_element_type.26
  3.2 1.0 scatter_custom_fusion.1
  4.2 0.7 all_to_all.17
  4.9 7.3 %all-to-all-start.1 = ((f32[1,32,8]{2,0,1:T(1,128)}), f32[1,32,8]{2,0,1:T(1,128)S(1)}, u32[]{:S(2)}, u32[]{:S(2)}) async-start(f32[1,32,8]{2,0,1:T(1,128)} %bitcast.9), calls=%async_computation.1 | async-start | bytes 32768 | tf_op jit(solution)/shard_map/all_to_all | solution.py:41
  12.3 1.7 %multiply_reduce_fusion = f32[64,128]{1,0:T(8,128)S(1)} fusion(f32[64,20,3,128]{3,0,2,1:T(8,128)} %param.9), kind=kLoop, calls=%fused_computation.14 | loop fusion | flops 974848 | bytes 1998848 | tf_op jit(solution)/shard_map/reduce_sum | solution.py:54
  14.0 0.1 copy.34
  14.1 4.7 %copy.35 = f32[64,60,128]{0,1,2:T(8,128)} copy(f32[64,60,128]{2,0,1:T(8,128)S(1)} %bitcast.22) | data formatting | bytes 3932160 | tf_op jit(solution)/shard_map/reshape | solution.py:67
  18.8 12.3 %fusion.4 = f32[60,60,128]{1,0,2:T(8,128)} fusion(f32[64,60,128]{0,1,2:T(8,128)} %copy.35, f32[64,128]{0,1:T(8,128)S(1)} %copy.34), kind=kOutput, calls=%fused_computation.12 | convolution fusion | flops 354385920 | bytes 3842048 | tf_op jit(solution)/shard_map/qme,qne->mne/dot_general | solution.py:16
  31.1 4.7 %copy.37 = f32[60,60,128]{2,1,0:T(8,128)} copy(f32[60,60,128]{1,0,2:T(8,128)} %fusion.4) | data formatting | bytes 3686400 | tf_op jit(solution)/shard_map/qme,qne->mne/transpose | solution.py:16
  35.9 3.0 %reshape.57 = f32[20,3,20,3,128]{4,3,2,1,0:T(4,128)S(1)} reshape(f32[60,60,128]{2,1,0:T(8,128)} %copy.37) | data formatting | bytes 3686400 | tf_op jit(solution)/shard_map/reshape | solution.py:19
  38.9 0.9 select_reduce_fusion
  39.8 0.5 fusion.3
  40.3 0.2 copy-done.4
  40.5 2.1 %copy.40 = f32[20,3,20,3,128]{4,3,2,1,0:T(4,128)} copy(f32[20,3,20,3,128]{4,2,3,1,0:T(8,128)S(1)} %fusion.3) | data formatting | bytes 3686400 | tf_op jit(solution)/shard_map/add | solution.py:22
  42.6 2.9 %reshape.58 = f32[3600,128]{1,0:T(8,128)S(1)} reshape(f32[20,3,20,3,128]{4,3,2,1,0:T(4,128)} %copy.40) | data formatting | bytes 3686400 | tf_op jit(solution)/shard_map/reshape | solution.py:26
  45.5 3.4 %gather_fusion = f32[1830,128]{1,0:T(8,128)S(1)} fusion(f32[3600,128]{1,0:T(8,128)S(1)} %reshape.58, s32[2048]{0:T(1024)S(1)} %pad_clamp_fusion.1), kind=kCustom, calls=%fused_computation | custom fusion | bytes 1881240 | tf_op jit(solution)/shard_map/jit(_take)/gather | solution.py:70
  48.9 0.3 copy.41
  49.3 2.5 %scatter_custom_fusion = f32[1830,256]{0,1:T(8,128)} fusion(s32[128]{0:T(128)S(1)} %fusion.14, f32[128,1830]{1,0:T(8,128)S(1)} %copy.41, f32[]{:T(128)} %constant.29.clone.1), kind=kCustom, calls=%fused_computation.15 | custom fusion | bytes 1873924 | tf_op jit(solution)/shard_map/scatter | solution.py:71
  51.8 5.8 %all-to-all-start = ((f32[1830,32,8]{0,2,1:T(8,128)}), f32[1830,32,8]{0,2,1:T(8,128)S(1)}, u32[]{:S(2)}, u32[]{:S(2)}) async-start(f32[1830,32,8]{0,2,1:T(8,128)} %bitcast.7), calls=%async_computation | async-start | bytes 3932160 | tf_op jit(solution)/shard_map/all_to_all | solution.py:40
  57.7 0.7 multiply_reduce_fusion.2
  58.3 65.9 %psum.7 = f32[]{:T(128)} all-reduce(f32[]{:T(128)} %multiply_reduce_fusion.2), channel_id=1, replica_groups=mesh['row'=8,'col'=4] {'row','col'}, use_global_device_ids=true, to_apply=%region_8.9 | all-reduce | flops 1 | bytes 8 | tf_op jit(solution)/shard_map/psum | solution.py:56
  124.9 0.1 convert_reduce_fusion
  125.0 0.1 convert_element_type.28
  125.1 1.3 copy-done.1
  126.4 1.8 %copy.42 = f32[1830,256]{1,0:T(8,128)S(1)} copy(f32[1830,256]{0,1:T(8,128)} %bitcast.23) | data formatting | bytes 3747840 | tf_op jit(solution)/shard_map/all_to_all | solution.py:40
  128.2 10.0 %gather_fusion.1 = f32[3600,256]{1,0:T(8,128)} fusion(f32[1830,256]{1,0:T(8,128)S(1)} %copy.42, s32[4096]{0:T(1024)S(1)} %pad_clamp_fusion), kind=kCustom, calls=%fused_computation.1 | custom fusion | bytes 7387200 | tf_op jit(solution)/shard_map/jit(_take)/gather | solution.py:73
  138.2 3.9 %convolution_divide_fusion = f32[3600,128]{1,0:T(8,128)S(1)} fusion(f32[3600,256]{1,0:T(8,128)} %gather_fusion.1, f32[]{:T(128)S(6)} %div.9, s32[256]{0:T(256)S(1)} %convert_element_type.28), kind=kOutput, calls=%fused_computation.6 | convolution fusion | flops 1416071168 | bytes 5530628 | tf_op jit(solution)/shard_map/dot_general | solution.py:78
  142.0 1.4 reshape.59
  (22 shorter events, 0.1 us)
Async XLA Ops:
  0.0 14.1 %copy-start = (f32[64,20,3,128]{3,0,2,1:T(8,128)S(1)}, f32[64,20,3,128]{3,0,2,1:T(8,128)}, u32[]{:S(2)}) copy-start(f32[64,20,3,128]{3,0,2,1:T(8,128)} %param.9) | copy-start | bytes 5898244
  0.0 14.0 %copy-start.7 = (s32[128]{0:T(128)S(1)}, s32[128]{0:T(128)}, u32[]{:S(2)}) copy-start(s32[128]{0:T(128)} %param.11) | copy-start | bytes 1540
  0.0 14.0 %copy-start.2 = (f32[64,128]{1,0:T(8,128)S(1)}, f32[64,128]{1,0:T(8,128)}, u32[]{:S(2)}) copy-start(f32[64,128]{1,0:T(8,128)} %param.10) | copy-start | bytes 98308
  4.9 46.9 %all-to-all-start.1 = ((f32[1,32,8]{2,0,1:T(1,128)}), f32[1,32,8]{2,0,1:T(1,128)S(1)}, u32[]{:S(2)}, u32[]{:S(2)}) async-start(f32[1,32,8]{2,0,1:T(1,128)} %bitcast.9), calls=%async_computation.1 | async-start | bytes 32768 | tf_op jit(solution)/shard_map/all_to_all | solution.py:41
  38.8 0.9 copy-start.5
  38.9 0.9 copy-start.6
  39.8 0.7 copy-start.4
  51.8 73.1 %copy-start.3 = (s32[3600]{0:T(1024)S(1)}, s32[3600]{0:T(1024)}, u32[]{:S(2)}) copy-start(s32[3600]{0:T(1024)} %constant.83) | copy-start | bytes 43204
  51.8 73.3 %all-to-all-start = ((f32[1830,32,8]{0,2,1:T(8,128)}), f32[1830,32,8]{0,2,1:T(8,128)S(1)}, u32[]{:S(2)}, u32[]{:S(2)}) async-start(f32[1830,32,8]{0,2,1:T(8,128)} %bitcast.7), calls=%async_computation | async-start | bytes 3932160 | tf_op jit(solution)/shard_map/all_to_all | solution.py:40
  125.1 1.3 copy-start.1
where the time goes:
time: 144 us; the launch traced here: 143 us
  blocking collectives  65.9 us (46%)
  local copies, waits for them, and re-layouts  40.2 us (28%)
  matrix products  16.2 us (11%)
  starting transfers between devices  13.2 us (9%)
  other arithmetic  7.07 us (5%)
    psum x1, blocking collectives, shards(): total = lax.psum(local_trace, ('row', 'col'))  65.9 us
    dot_general x1, matrix products, stiffness(): jnp.einsum('qme,qne->mne', gflat * weff[:, None, :], gflat, precision=lax...  12.3 us
    gather x1, local copies, waits for them, and re-layouts, shards(): received = jnp.take(moved, jnp.asarray(mirror_index, jnp.int32), axis=0)  9.98 us
    all_to_all x1, starting transfers between devices, deliver(): lax.all_to_all(slotcol, ('row', 'col'), split_axis=1, concat_axis=1, tile...  7.33 us
    all_to_all x1, starting transfers between devices, deliver(): lax.all_to_all(payload, ('row', 'col'), split_axis=1, concat_axis=1, tile...  5.83 us
    transpose x1, local copies, waits for them, and re-layouts, stiffness(): jnp.einsum('qme,qne->mne', gflat * weff[:, None, :], gflat, precision=lax...  4.73 us
    reshape x1, local copies, waits for them, and re-layouts, shards(): gflat = grads.reshape(Q, NDOF, count)  4.68 us
    dot_general x1, matrix products, shards(): jnp.dot(received, placing, precision=lax.Precision.HIGHEST, preferred_ele...  3.85 us
  transfers between devices with their start and end apart: 2, of which 0 were waited for; matrix products, arithmetic and copies ran while one was open for 28% of the time, Pallas kernels for 0%

commit v1 on v0

v1 whole, which is shorter than its diff:
```python
import functools

import jax
import jax.numpy as jnp
from jax import lax
from jax.experimental import pallas as pl
from jax.experimental.pallas import tpu as pltpu
from jax.sharding import PartitionSpec as P

GP = 8
LANES = 128
CHUNKS = 3
F32 = jnp.float32
BF16 = jnp.bfloat16
NT = (((1,), (1,)), ((), ()))


def split2(x):
    high = x.astype(BF16)
    return high, (x - high.astype(F32)).astype(BF16)


def row_base(d, nodes, pair):
    half = nodes // 2
    if d < half:
        return d * 9 * nodes + pair * nodes, nodes
    return half * 9 * nodes + pair * half, half


def send_kernel(sizes, grads, weights, counts, lame, shear, owner, slot, recv,
                gbuf, wbuf, kbuf, send, ssem, rsem, lsem):
    nodes, nq, nrow, ncol, cap, packed, total_rows = sizes
    ndev = nrow * ncol
    width = ndev * cap
    half = nodes // 2
    clen = total_rows // CHUNKS
    me = lax.axis_index("row") * ncol + lax.axis_index("col")

    def device(k):
        t = lax.rem(me + k, ndev)
        return t, (t // ncol, lax.rem(t, ncol))

    barrier = pltpu.get_barrier_semaphore()

    @pl.loop(1, ndev)
    def _(k):
        pl.semaphore_signal(barrier, inc=1, device_id=device(k)[1],
                            device_id_type=pl.DeviceIdType.MESH)

    span = 2 * nodes
    pad = 24

    def prepare(q, carry):
        weight = weights[pl.ds(q, 1), :]
        weight = jnp.where(q < counts[...] * GP, weight, 0.0)
        for i in range(3):
            values = grads[pl.ds(i * nq + q, nodes, stride=3 * nq), :]
            gbuf[q, pl.ds(i * span, nodes), :] = values
            gbuf[q, pl.ds(i * span + nodes, nodes), :] = values
            wbuf[q, pl.ds(i * pad, nodes), :] = values * weight
        return carry

    lax.fori_loop(0, nq, prepare, 0, unroll=4)

    who = owner[...].astype(F32)
    across = jnp.broadcast_to(who, (LANES, LANES))
    down = across.T
    first = lax.broadcasted_iota(jnp.int32, (LANES, LANES), 0)
    second = lax.broadcasted_iota(jnp.int32, (LANES, LANES), 1)
    same = jnp.where((across == down) & (first < second), 1.0, 0.0)
    rank = jnp.sum(same, axis=0, keepdims=True)
    position = (who * cap + rank).astype(jnp.int32)
    where = lax.broadcasted_iota(jnp.int32, (width, LANES), 0)
    onehot = jnp.where(where == position, 1.0, 0.0).astype(BF16)
    onehot2 = jnp.concatenate([onehot, onehot], axis=1)

    lam, mu = lame[...], shear[...]
    trace_row = jnp.zeros((1, LANES), F32)
    tail = total_rows - packed
    extra = lax.broadcasted_iota(jnp.int32, (tail, LANES), 0)
    kbuf[pl.ds(packed, tail), :] = jnp.where(extra == 0, slot[...].astype(F32) + 1.0, 0.0)

    chunk = 0
    for d in range(half + 1):
        tiles = 3 if d < half else 2

        def step(q, acc, d=d, tiles=tiles):
            acc = list(acc)
            for t in range(tiles):
                left = [wbuf[q, pl.ds(i * pad + 8 * t, 8), :] for i in range(3)]
                right = [gbuf[q, pl.ds(j * span + d + 8 * t, 8), :] for j in range(3)]
                for i in range(3):
                    for j in range(3):
                        n = t * 9 + 3 * i + j
                        acc[n] = acc[n] + left[i] * right[j]
            return tuple(acc)

        zero = jnp.zeros((8, LANES), F32)
        acc = lax.fori_loop(0, nq, step, (zero,) * (9 * tiles), unroll=2)
        for t in range(tiles):
            m = acc[9 * t: 9 * t + 9]
            diag = m[0] + m[4] + m[8]
            _, length = row_base(d, nodes, 0)
            rows = min(8, length - 8 * t)
            if d == 0:
                trace_row = trace_row + jnp.sum(diag[:rows], axis=0, keepdims=True)
            for i in range(3):
                for j in range(3):
                    value = lam * m[3 * i + j] + mu * m[3 * j + i]
                    if i == j:
                        value = value + mu * diag
                    base, _ = row_base(d, nodes, 3 * i + j)
                    kbuf[pl.ds(base + 8 * t, rows), :] = value[:rows]
        if d == 0:
            local = jnp.sum((lam + 4.0 * mu) * trace_row, axis=(0, 1), keepdims=True)
        done = packed if d == half else 9 * nodes * (d + 1)
        while chunk < CHUNKS and (done >= (chunk + 1) * clen or d == half):
            high, low = split2(kbuf[pl.ds(chunk * clen, clen), :])
            both = jnp.concatenate([high, low], axis=1)
            out = lax.dot_general(onehot2, both, NT, preferred_element_type=F32)
            if chunk == CHUNKS - 1:
                column = lax.broadcasted_iota(jnp.int32, (width, clen), 1)
                out = jnp.where(column == packed + 1 - chunk * clen, local, out)
            send[chunk] = out
            if chunk == 0:
                pl.semaphore_wait(barrier, ndev - 1)

            @pl.loop(1, ndev)
            def _(k, chunk=chunk):
                t, where_to = device(k)
                pltpu.make_async_remote_copy(
                    src_ref=send.at[chunk, pl.ds(pl.multiple_of(t * cap, 8), cap)],
                    dst_ref=recv.at[chunk, pl.ds(pl.multiple_of(me * cap, 8), cap)],
                    send_sem=ssem.at[chunk], recv_sem=rsem.at[chunk],
                    device_id=where_to, device_id_type=pl.DeviceIdType.MESH).start()

            mine = pl.ds(pl.multiple_of(me * cap, 8), cap)
            pltpu.make_async_copy(send.at[chunk, mine], recv.at[chunk, mine],
                                  lsem.at[chunk]).start()
            chunk += 1

    for c in range(CHUNKS):
        mine = pl.ds(pl.multiple_of(me * cap, 8), cap)
        pltpu.make_async_copy(send.at[c, mine], recv.at[c, mine], lsem.at[c]).wait()
        most = pl.ds(0, (ndev - 1) * cap)
        pltpu.make_async_copy(send.at[c, most], send.at[c, most], ssem.at[c]).wait()
        pltpu.make_async_copy(recv.at[c, most], recv.at[c, most], rsem.at[c]).wait()


def place_kernel(sizes, recv, out, tbuf):
    nodes, ndof, cap, packed, total_rows, count_all = sizes
    clen = total_rows // CHUNKS
    half = nodes // 2
    pitch = ndof + (-ndof) % 8
    last = recv[CHUNKS - 1]
    start = (packed - (CHUNKS - 1) * clen) // LANES * LANES
    inner = packed - (CHUNKS - 1) * clen - start
    info = last[:, start:start + LANES]
    width = info.shape[0]
    slots = info[:, inner:inner + 1]
    total = jnp.sum(info[:, inner + 1:inner + 2], axis=0, keepdims=True) / cap
    inverse = (ndof * count_all) / total
    lane = lax.broadcasted_iota(jnp.int32, (width, LANES), 1)
    placing = jnp.where(slots.astype(jnp.int32) == lane + 1, 1.0, 0.0)
    placing = placing.T.astype(BF16)
    for c in range(CHUNKS):
        high, low = split2(recv[c])
        summed = jnp.dot(placing, high, preferred_element_type=F32)
        summed = summed + jnp.dot(placing, low, preferred_element_type=F32)
        tbuf[pl.ds(c * clen, clen), :] = (summed * inverse).T
    for d in range(half + 1):
        for i in range(3):
            for j in range(3):
                base, length = row_base(d, nodes, 3 * i + j)
                pieces = [(0, min(length, nodes - d), d)]
                if length > nodes - d:
                    pieces.append((nodes - d, length, d - nodes))
                for begin, end, shift in pieces:
                    for a in range(begin, end, 8):
                        n = min(8, end - a)
                        value = tbuf[pl.ds(base + a, n), :]
                        m0, n0 = 3 * a + i, 3 * (a + shift) + j
                        stride = 3 * pitch + 3
                        if n == 1:
                            out[pl.ds(m0 * pitch + n0, 1), :] = value
                            out[pl.ds(n0 * pitch + m0, 1), :] = value
                        else:
                            out[pl.ds(m0 * pitch + n0, n, stride=stride), :] = value
                            if d > 0:
                                out[pl.ds(n0 * pitch + m0, n, stride=stride), :] = value


def shards(nrow, ncol, grads, weights, counts, lame_first, shear, dest_owner, dest_slot):
    nq, nodes, _, count = grads.shape
    ndev = nrow * ncol
    ndof = 3 * nodes
    cap = max(2, 2 * count // ndev)
    cap = cap + (-cap) % 8
    width = ndev * cap
    half = nodes // 2
    packed = 9 * nodes * half + 9 * half
    unit = LANES * CHUNKS
    total_rows = packed + 2
    total_rows = total_rows + (-total_rows) % unit
    clen = total_rows // CHUNKS
    pitch = ndof + (-ndof) % 8
    gview = jnp.transpose(grads, (1, 2, 0, 3)).reshape(ndof * nq, count)
    row = lambda x: x.reshape(1, count)
    vmem = pl.BlockSpec(memory_space=pltpu.VMEM)
    recv = pl.pallas_call(
        functools.partial(send_kernel, (nodes, nq, nrow, ncol, cap, packed, total_rows)),
        out_shape=jax.ShapeDtypeStruct((CHUNKS, width, clen), F32),
        in_specs=[vmem] * 7,
        out_specs=vmem,
        scratch_shapes=[
            pltpu.VMEM((nq, 6 * nodes, LANES), F32),
            pltpu.VMEM((nq, 72, LANES), F32),
            pltpu.VMEM((total_rows, LANES), F32),
            pltpu.VMEM((CHUNKS, width, clen), F32),
            pltpu.SemaphoreType.DMA((CHUNKS,)),
            pltpu.SemaphoreType.DMA((CHUNKS,)),
            pltpu.SemaphoreType.DMA((CHUNKS,)),
        ],
        compiler_params=pltpu.CompilerParams(
            collective_id=0, has_side_effects=True, vmem_limit_bytes=56 << 20),
        name="moments_send",
    )(gview, weights, row(counts), row(lame_first), row(shear), row(dest_owner), row(dest_slot))
    out = pl.pallas_call(
        functools.partial(place_kernel, (nodes, ndof, cap, packed, total_rows, count * ndev)),
        out_shape=jax.ShapeDtypeStruct((ndof * pitch, LANES), F32),
        in_specs=[vmem],
        out_specs=vmem,
        scratch_shapes=[pltpu.VMEM((total_rows, LANES), F32)],
        compiler_params=pltpu.CompilerParams(vmem_limit_bytes=56 << 20),
        name="place",
    )(recv)
    return out.reshape(ndof, pitch, LANES)[:, :ndof, :]


def solution(mesh):
    both = ("row", "col")
    in_specs = (P(None, None, None, both), P(None, both), P(both), P(both), P(both),
                P(both, None), P(both))
    body = functools.partial(shards, mesh.shape["row"], mesh.shape["col"])
    return jax.shard_map(body, mesh=mesh, in_specs=in_specs, out_specs=P(None, None, both),
                         check_vma=False)
```

time: 144 us -> 57.5 us (0.40)
  the two profiles are of different devices: /device:TPU:0 before, /device:TPU:13 now
where the time goes in v1:
time: 57.5 us; the launch traced here: 57.4 us
  Pallas kernels  57.4 us (100%)
    pallas_call x1, Pallas kernels, shards(): pl.pallas_call(functools.partial(send_kernel, (nodes, nq, nrow, ncol, cap...  53.7 us
    pallas_call x1, Pallas kernels, shards(): pl.pallas_call(functools.partial(place_kernel, (nodes, ndof, cap, packed,...  3.62 us

profile of v1, /device:TPU:13, one launch (start us, length us, event | category | flops | bytes accessed | tf_op | source)
XLA Modules:
  0.0 57.4 jit_solution(16834068190516083133)
XLA Ops:
  0.0 53.7 %moments_send.1.recv = f32[3,256,640]{2,1,0:T(8,128)} custom-call(f32[3840,128]{1,0:T(8,128)} %bitcast.10, f32[64,128]{1,0:T(8,128)} %weights.1, s32[1,128]{1,0:T(1,128)} %bitcast.12, f32[1,128]{1,0:T(1,128)} %bitcast.13, f32[1,128]{1,0:T(1,128)} %bitcast.14, s32[1,128]{1,0:T(1,128)} %bitcast.15, s32[1,128]{1,0:T(1,128)} %bitcast.16), custom_call_target="tpu_custom_call" | custom-call | tf_op jit(solution)/shard_map/moments_send/pallas_call | solution.py:210
  53.8 3.6 %place.1 = f32[3840,128]{1,0:T(8,128)} custom-call(f32[3,256,640]{2,1,0:T(8,128)} %moments_send.1.recv), custom_call_target="tpu_custom_call" | custom-call | tf_op jit(solution)/shard_map/place/pallas_call | solution.py:228

commit v2 on v1

v2 whole, which is shorter than its diff:
```python
import functools

import jax
import jax.numpy as jnp
from jax import lax
from jax.experimental import pallas as pl
from jax.experimental.pallas import tpu as pltpu
from jax.sharding import PartitionSpec as P

GP = 8
LANES = 128
HEAD = 8
TILES = (1, 2, 4, 6)
F32 = jnp.float32
BF16 = jnp.bfloat16
NT = (((1,), (1,)), ((), ()))


def split2(x):
    high = x.astype(BF16)
    return high, (x - high.astype(F32)).astype(BF16)


def row_base(d, nodes, i, j):
    half = nodes // 2
    if d == 0:
        i, j = min(i, j), max(i, j)
        return HEAD + (3 * i - i * (i + 1) // 2 + j) * nodes, nodes
    start = HEAD + 6 * nodes + (d - 1) * 9 * nodes
    if d < half:
        return start + (3 * i + j) * nodes, nodes
    return start + (3 * i + j) * half, half


def chunk_bounds(total_rows):
    cuts = [0]
    for tiles in TILES:
        if cuts[-1] + tiles * LANES < total_rows:
            cuts.append(cuts[-1] + tiles * LANES)
    return tuple(zip(cuts, cuts[1:] + [total_rows]))


def send_kernel(sizes, grads, weights, counts, lame, shear, owner, slot, sums,
                gbuf, wbuf, kbuf, send, recv, ssem, rsem, lsem):
    nodes, nq, nrow, ncol, cap, packed, total_rows, count_all = sizes
    ndev = nrow * ncol
    width = ndev * cap
    half = nodes // 2
    chunks = chunk_bounds(total_rows)
    me = lax.axis_index("row") * ncol + lax.axis_index("col")
    mine = pl.ds(pl.multiple_of(me * cap, 8), cap)
    most = pl.ds(0, (ndev - 1) * cap)

    def device(k):
        t = lax.rem(me + k, ndev)
        return t, (t // ncol, lax.rem(t, ncol))

    barrier = pltpu.get_barrier_semaphore()

    @pl.loop(1, ndev)
    def _(k):
        pl.semaphore_signal(barrier, inc=1, device_id=device(k)[1],
                            device_id_type=pl.DeviceIdType.MESH)

    span = 2 * nodes
    pad = 24

    def prepare(q, carry):
        weight = weights[pl.ds(q, 1), :]
        weight = jnp.where(q < counts[...] * GP, weight, 0.0)
        for i in range(3):
            values = grads[pl.ds(i * nq + q, nodes, stride=3 * nq), :]
            gbuf[q, pl.ds(i * span, nodes), :] = values
            gbuf[q, pl.ds(i * span + nodes, nodes), :] = values
            wbuf[q, pl.ds(i * pad, nodes), :] = values * weight
        return carry

    lax.fori_loop(0, nq, prepare, 0, unroll=4)

    who = owner[...].astype(F32)
    across = jnp.broadcast_to(who, (LANES, LANES))
    down = across.T
    first = lax.broadcasted_iota(jnp.int32, (LANES, LANES), 0)
    second = lax.broadcasted_iota(jnp.int32, (LANES, LANES), 1)
    same = jnp.where((across == down) & (first < second), 1.0, 0.0)
    rank = jnp.sum(same, axis=0, keepdims=True)
    position = (who * cap + rank).astype(jnp.int32)
    where = lax.broadcasted_iota(jnp.int32, (width, LANES), 0)
    onehot = jnp.where(where == position, 1.0, 0.0).astype(BF16)
    onehot2 = jnp.concatenate([onehot, onehot], axis=1)

    lam, mu = lame[...], shear[...]
    trace_row = jnp.zeros((1, LANES), F32)
    extra = lax.broadcasted_iota(jnp.int32, (HEAD, LANES), 0)
    kbuf[pl.ds(0, HEAD), :] = jnp.where(extra == 0, slot[...].astype(F32) + 1.0, 0.0)
    kbuf[pl.ds(packed, total_rows - packed), :] = jnp.zeros((total_rows - packed, LANES), F32)

    chunk = 0
    for d in range(half + 1):
        tiles = 3 if d < half else 2

        def step(q, acc, d=d, tiles=tiles):
            acc = list(acc)
            for t in range(tiles):
                left = [wbuf[q, pl.ds(i * pad + 8 * t, 8), :] for i in range(3)]
                right = [gbuf[q, pl.ds(j * span + d + 8 * t, 8), :] for j in range(3)]
                for i in range(3):
                    for j in range(3):
                        n = t * 9 + 3 * i + j
                        acc[n] = acc[n] + left[i] * right[j]
            return tuple(acc)

        zero = jnp.zeros((8, LANES), F32)
        acc = lax.fori_loop(0, nq, step, (zero,) * (9 * tiles), unroll=2)
        for t in range(tiles):
            m = acc[9 * t: 9 * t + 9]
            diag = m[0] + m[4] + m[8]
            _, length = row_base(d, nodes, 0, 0)
            rows = min(8, length - 8 * t)
            if d == 0:
                trace_row = trace_row + jnp.sum(diag[:rows], axis=0, keepdims=True)
            for i in range(3):
                for j in range(i if d == 0 else 0, 3):
                    value = lam * m[3 * i + j] + mu * m[3 * j + i]
                    if i == j:
                        value = value + mu * diag
                    base, _ = row_base(d, nodes, i, j)
                    kbuf[pl.ds(base + 8 * t, rows), :] = value[:rows]
        if d == 0:
            local = jnp.sum((lam + 4.0 * mu) * trace_row, axis=(0, 1), keepdims=True)
        done = total_rows if d == half else HEAD + 6 * nodes + 9 * nodes * d
        while chunk < len(chunks) and chunks[chunk][1] <= done:
            low_row, high_row = chunks[chunk]
            columns = pl.ds(low_row, high_row - low_row)
            high, low = split2(kbuf[columns, :])
            both = jnp.concatenate([high, low], axis=1)
            out = lax.dot_general(onehot2, both, NT, preferred_element_type=F32)
            if chunk == 0:
                column = lax.broadcasted_iota(jnp.int32, out.shape, 1)
                out = jnp.where(column == 1, local, out)
            send[:, columns] = out
            if chunk == 0:
                pl.semaphore_wait(barrier, ndev - 1)

            @pl.loop(1, ndev)
            def _(k, chunk=chunk, columns=columns):
                t, where_to = device(k)
                pltpu.make_async_remote_copy(
                    src_ref=send.at[pl.ds(pl.multiple_of(t * cap, 8), cap), columns],
                    dst_ref=recv.at[mine, columns],
                    send_sem=ssem.at[chunk], recv_sem=rsem.at[chunk],
                    device_id=where_to, device_id_type=pl.DeviceIdType.MESH).start()

            pltpu.make_async_copy(send.at[mine, columns], recv.at[mine, columns],
                                  lsem.at[chunk]).start()
            chunk += 1

    for c, (low_row, high_row) in enumerate(chunks):
        columns = pl.ds(low_row, high_row - low_row)
        pltpu.make_async_copy(send.at[mine, columns], recv.at[mine, columns], lsem.at[c]).wait()
        pltpu.make_async_copy(recv.at[most, columns], recv.at[most, columns], rsem.at[c]).wait()
        if c == 0:
            info = recv[:, 0:LANES]
            total = jnp.sum(info[:, 1:2], axis=0, keepdims=True) / cap
            inverse = (3 * nodes * count_all) / total
            lane = lax.broadcasted_iota(jnp.int32, (width, LANES), 1)
            placing = jnp.where(info[:, 0:1].astype(jnp.int32) == lane + 1, 1.0, 0.0)
            placing = placing.T.astype(BF16)
        high, low = split2(recv[:, columns])
        summed = jnp.dot(placing, high, preferred_element_type=F32)
        summed = summed + jnp.dot(placing, low, preferred_element_type=F32)
        sums[columns, :] = (summed * inverse).T
    for c, (low_row, high_row) in enumerate(chunks):
        columns = pl.ds(low_row, high_row - low_row)
        pltpu.make_async_copy(send.at[most, columns], send.at[most, columns], ssem.at[c]).wait()


def mirror_kernel(nodes, sums, out):
    half = nodes // 2
    ndof = 3 * nodes
    pitch = ndof + (-ndof) % 8
    for d in range(half + 1):
        for i in range(3):
            for j in range(3):
                base, length = row_base(d, nodes, i, j)
                pieces = [(0, min(length, nodes - d), d)]
                if length > nodes - d:
                    pieces.append((nodes - d, length, d - nodes))
                for begin, end, shift in pieces:
                    for a in range(begin, end, 8):
                        n = min(8, end - a)
                        value = sums[pl.ds(base + a, n), :]
                        m0, n0 = 3 * a + i, 3 * (a + shift) + j
                        stride = 3 * pitch + 3
                        if n == 1:
                            out[pl.ds(m0 * pitch + n0, 1), :] = value
                            out[pl.ds(n0 * pitch + m0, 1), :] = value
                        else:
                            out[pl.ds(m0 * pitch + n0, n, stride=stride), :] = value
                            if d > 0:
                                out[pl.ds(n0 * pitch + m0, n, stride=stride), :] = value


def shards(nrow, ncol, grads, weights, counts, lame_first, shear, dest_owner, dest_slot):
    nq, nodes, _, count = grads.shape
    ndev = nrow * ncol
    ndof = 3 * nodes
    cap = max(2, 2 * count // ndev)
    cap = cap + (-cap) % 8
    width = ndev * cap
    half = nodes // 2
    packed = HEAD + 6 * nodes + 9 * nodes * (half - 1) + 9 * half
    total_rows = packed + (-packed) % LANES
    pitch = ndof + (-ndof) % 8
    gview = jnp.transpose(grads, (1, 2, 0, 3)).reshape(ndof * nq, count)
    row = lambda x: x.reshape(1, count)
    vmem = pl.BlockSpec(memory_space=pltpu.VMEM)
    steps = len(chunk_bounds(total_rows))
    sizes = (nodes, nq, nrow, ncol, cap, packed, total_rows, count * ndev)
    sums = pl.pallas_call(
        functools.partial(send_kernel, sizes),
        out_shape=jax.ShapeDtypeStruct((total_rows, LANES), F32),
        in_specs=[vmem] * 7,
        out_specs=vmem,
        scratch_shapes=[
            pltpu.VMEM((nq, 6 * nodes, LANES), F32),
            pltpu.VMEM((nq, 72, LANES), F32),
            pltpu.VMEM((total_rows, LANES), F32),
            pltpu.VMEM((width, total_rows), F32),
            pltpu.VMEM((width, total_rows), F32),
            pltpu.SemaphoreType.DMA((steps,)),
            pltpu.SemaphoreType.DMA((steps,)),
            pltpu.SemaphoreType.DMA((steps,)),
        ],
        compiler_params=pltpu.CompilerParams(
            collective_id=0, has_side_effects=True, vmem_limit_bytes=56 << 20),
        name="moments_exchange",
    )(gview, weights, row(counts), row(lame_first), row(shear), row(dest_owner), row(dest_slot))
    out = pl.pallas_call(
        functools.partial(mirror_kernel, nodes),
        out_shape=jax.ShapeDtypeStruct((ndof * pitch, LANES), F32),
        in_specs=[vmem],
        out_specs=vmem,
        compiler_params=pltpu.CompilerParams(vmem_limit_bytes=56 << 20),
        name="mirror",
    )(sums)
    return out.reshape(ndof, pitch, LANES)[:, :ndof, :]


def solution(mesh):
    both = ("row", "col")
    in_specs = (P(None, None, None, both), P(None, both), P(both), P(both), P(both),
                P(both, None), P(both))
    body = functools.partial(shards, mesh.shape["row"], mesh.shape["col"])
    return jax.shard_map(body, mesh=mesh, in_specs=in_specs, out_specs=P(None, None, both),
                         check_vma=False)
```

time: 57.5 us -> 55.7 us (0.969)
  the two profiles are of different devices: /device:TPU:13 before, /device:TPU:0 now
where the time goes in v2:
time: 55.7 us; the launch traced here: 55.5 us
  Pallas kernels  55.5 us (100%)
    pallas_call x1, Pallas kernels, shards(): pl.pallas_call(functools.partial(send_kernel, sizes), out_shape=jax.Shape...  52.9 us
    pallas_call x1, Pallas kernels, shards(): pl.pallas_call(functools.partial(mirror_kernel, nodes), out_shape=jax.Sha...  2.65 us

profile of v2, /device:TPU:0, one launch (start us, length us, event | category | flops | bytes accessed | tf_op | source)
XLA Modules:
  0.0 55.5 jit_solution(14883373442994022158)
XLA Ops:
  0.0 52.9 %moments_exchange.1.sums = f32[1920,128]{1,0:T(8,128)} custom-call(f32[3840,128]{1,0:T(8,128)} %bitcast.10, f32[64,128]{1,0:T(8,128)} %weights.1, s32[1,128]{1,0:T(1,128)} %bitcast.12, f32[1,128]{1,0:T(1,128)} %bitcast.13, f32[1,128]{1,0:T(1,128)} %bitcast.14, s32[1,128]{1,0:T(1,128)} %bitcast.15, s32[1,128]{1,0:T(1,128)} %bitcast.16), custom_call_target="tpu_custom_call" | custom-call | tf_op jit(solution)/shard_map/moments_exchange/pallas_call | solution.py:220
  52.9 2.6 %mirror.1 = f32[3840,128]{1,0:T(8,128)} custom-call(f32[1920,128]{1,0:T(8,128)} %moments_exchange.1.sums), custom_call_target="tpu_custom_call" | custom-call | tf_op jit(solution)/shard_map/mirror/pallas_call | solution.py:239

commit v3 on v2

--- a/solution.py
+++ b/solution.py
@@ -10,6 +10,7 @@
 GP = 8
 LANES = 128
 HEAD = 8
+BLOCKS = 4
 TILES = (1, 2, 4, 6)
 F32 = jnp.float32
 BF16 = jnp.bfloat16
@@ -175,30 +176,43 @@
         pltpu.make_async_copy(send.at[most, columns], send.at[most, columns], ssem.at[c]).wait()
 
 
-def mirror_kernel(nodes, sums, out):
+def mirror_kernel(nodes, sums, out, obuf, osem):
     half = nodes // 2
     ndof = 3 * nodes
     pitch = ndof + (-ndof) % 8
-    for d in range(half + 1):
-        for i in range(3):
-            for j in range(3):
-                base, length = row_base(d, nodes, i, j)
-                pieces = [(0, min(length, nodes - d), d)]
-                if length > nodes - d:
-                    pieces.append((nodes - d, length, d - nodes))
-                for begin, end, shift in pieces:
-                    for a in range(begin, end, 8):
-                        n = min(8, end - a)
-                        value = sums[pl.ds(base + a, n), :]
-                        m0, n0 = 3 * a + i, 3 * (a + shift) + j
-                        stride = 3 * pitch + 3
-                        if n == 1:
-                            out[pl.ds(m0 * pitch + n0, 1), :] = value
-                            out[pl.ds(n0 * pitch + m0, 1), :] = value
-                        else:
-                            out[pl.ds(m0 * pitch + n0, n, stride=stride), :] = value
+    stride = 3 * pitch + 3
+    block = nodes // BLOCKS
+    copies = []
+
+    def move(source, m0, n0, n):
+        value = sums[pl.ds(source, n), :]
+        if n == 1:
+            obuf[pl.ds(m0 * pitch + n0, 1), :] = value
+        else:
+            obuf[pl.ds(m0 * pitch + n0, n, stride=stride), :] = value
+
+    for first in range(0, nodes, block):
+        for d in range(half + 1):
+            for i in range(3):
+                for j in range(3):
+                    base, length = row_base(d, nodes, i, j)
+                    for low, high, shift in ((0, nodes - d, d), (nodes - d, nodes, d - nodes)):
+                        high = min(high, length)
+                        begin, end = max(low, first), min(high, first + block)
+                        for a in range(begin, end, 8):
+                            n = min(8, end - a)
+                            move(base + a, 3 * a + i, 3 * (a + shift) + j, n)
+                        begin, end = max(low, first - shift), min(high, first - shift + block)
+                        for a in range(begin, end, 8):
+                            n = min(8, end - a)
                             if d > 0:
-                                out[pl.ds(n0 * pitch + m0, n, stride=stride), :] = value
+                                move(base + a, 3 * (a + shift) + j, 3 * a + i, n)
+        rows = pl.ds(3 * first * pitch, 3 * block * pitch)
+        copy = pltpu.make_async_copy(obuf.at[rows], out.at[rows], osem.at[first // block])
+        copy.start()
+        copies.append(copy)
+    for copy in copies:
+        copy.wait()
 
 
 def shards(nrow, ncol, grads, weights, counts, lame_first, shear, dest_owner, dest_slot):
@@ -219,7 +233,7 @@
     sizes = (nodes, nq, nrow, ncol, cap, packed, total_rows, count * ndev)
     sums = pl.pallas_call(
         functools.partial(send_kernel, sizes),
-        out_shape=jax.ShapeDtypeStruct((total_rows, LANES), F32),
+        out_shape=pltpu.VMEM((total_rows, LANES), F32),
         in_specs=[vmem] * 7,
         out_specs=vmem,
         scratch_shapes=[
@@ -240,10 +254,11 @@
         functools.partial(mirror_kernel, nodes),
         out_shape=jax.ShapeDtypeStruct((ndof * pitch, LANES), F32),
         in_specs=[vmem],
-        out_specs=vmem,
+        out_specs=pl.BlockSpec(memory_space=pl.ANY),
+        scratch_shapes=[pltpu.VMEM((ndof * pitch, LANES), F32), pltpu.SemaphoreType.DMA((BLOCKS,))],
         compiler_params=pltpu.CompilerParams(vmem_limit_bytes=56 << 20),
         name="mirror",
-    )(sums)
+    )(pltpu.with_memory_space_constraint(sums, pltpu.VMEM))
     return out.reshape(ndof, pitch, LANES)[:, :ndof, :]
 
 

time: 55.7 us -> 53.5 us (0.961)
  Pallas kernels: 55.5 us -> 53.3 us
    pallas_call x1, Pallas kernels: 2.65 us -> 1.4 us  [shards(): pl.pallas_call(functools.partial(mirror_kernel, nodes), out_shape=jax.Sha...]
    pallas_call x1, Pallas kernels: 52.9 us -> 51.9 us  [shards(): pl.pallas_call(functools.partial(send_kernel, sizes), out_shape=pltpu.VME...]
where the time goes in v3:
time: 53.5 us; the launch traced here: 53.3 us
  Pallas kernels  53.3 us (100%)
    pallas_call x1, Pallas kernels, shards(): pl.pallas_call(functools.partial(send_kernel, sizes), out_shape=pltpu.VME...  51.9 us
    pallas_call x1, Pallas kernels, shards(): pl.pallas_call(functools.partial(mirror_kernel, nodes), out_shape=jax.Sha...  1.4 us

profile of v3, /device:TPU:0, one launch (start us, length us, event | category | flops | bytes accessed | tf_op | source)
XLA Modules:
  0.0 53.3 jit_solution(4782411476465450238)
XLA Ops:
  0.0 51.9 %moments_exchange.1.sums = f32[1920,128]{1,0:T(8,128)S(1)} custom-call(f32[3840,128]{1,0:T(8,128)} %bitcast.10, f32[64,128]{1,0:T(8,128)} %weights.1, s32[1,128]{1,0:T(1,128)} %bitcast.12, f32[1,128]{1,0:T(1,128)} %bitcast.13, f32[1,128]{1,0:T(1,128)} %bitcast.14, s32[1,128]{1,0:T(1,128)} %bitcast.15, s32[1,128]{1,0:T(1,128)} %bitcast.16), custom_call_target="tpu_custom_call" | custom-call | tf_op jit(solution)/shard_map/moments_exchange/pallas_call | solution.py:234
  51.9 1.4 %mirror.1 = f32[3840,128]{1,0:T(8,128)} custom-call(f32[1920,128]{1,0:T(8,128)S(1)} %moments_exchange.1.sums), custom_call_target="tpu_custom_call" | custom-call | tf_op jit(solution)/shard_map/mirror/pallas_call | solution.py:253
